TPU v7x, 32 devices: a whole 2x2x4 slice. The times are simulated.
32 devices in a mesh: row: 16 (over z, y, core), rows: 2 (over x).
Axes of the slice: x: 2, y: 2, z: 4, core: 2. Of those that a mesh axis runs over, the one named last changes fastest.
Arguments:
- hopping: float32 [2, 128, 512, 512], P(None, 'row', 'rows'), may hold values from -0.5 to 0.5
- lattice: int32 [3, 128], replicated, may hold values from -4 to 4
- kgrid: int32 [3, 32], replicated, may hold values from 0 to 7
- tangent: float32 [3, 32], replicated, may hold values from -4 to 4
- states: float32 [2, 32, 1024, 512], P(None, 'row'), may hold values from -6 to 6
Outputs:
- energies: float32 [32, 1024], P('row')
- velocities: float32 [32, 1024], P('row')
All inputs are finite; a program needn't handle non-finite values.
Results may differ from a plain program's by a relative error of at most 0.000075.
Values sent between devices are 32-bit elements; how exact they have to be, the bound alone decides.
A program may use at most 256 MiB of HBM per device.

v0:
```python
import math

import jax
import jax.numpy as jnp
from jax import lax
from jax.sharding import PartitionSpec as P

KGRID = 8


def phases(kgrid, lattice, tangent):
    turns = jnp.mod(jnp.sum(kgrid[:, :, None] * lattice[:, None, :], axis=0), KGRID)
    angle = turns.astype(jnp.float32) * (2.0 * math.pi / KGRID)
    weight = jnp.sum(tangent[:, :, None] * lattice[:, None, :].astype(jnp.float32), axis=0)
    return (jnp.cos(angle), jnp.sin(angle), weight)


def project(m_re, m_im, rows, cols):
    high = lax.Precision.HIGH
    y_re = jnp.einsum("kmac,kic->kmai", m_re, cols[0], precision=high) - jnp.einsum(
        "kmac,kic->kmai", m_im, cols[1], precision=high
    )
    y_im = jnp.einsum("kmac,kic->kmai", m_re, cols[1], precision=high) + jnp.einsum(
        "kmac,kic->kmai", m_im, cols[0], precision=high
    )
    a = jnp.swapaxes(rows[0], 1, 2)[:, None]
    b = jnp.swapaxes(rows[1], 1, 2)[:, None]
    return jnp.sum(a * y_re + b * y_im, axis=2)


def per_device(hopping, lattice, kgrid, tangent, states):
    row_count = hopping.shape[2]
    row_start = lax.axis_index("rows") * row_count
    state_rows = lax.dynamic_slice_in_dim(states, row_start, row_count, 3)
    cosine, sine, weight = phases(kgrid, lattice, tangent)
    first_d, second_d = -weight * sine, weight * cosine
    coef = jnp.stack(
        [
            jnp.stack([cosine, -sine], axis=1),
            jnp.stack([sine, cosine], axis=1),
            jnp.stack([first_d, -second_d], axis=1),
            jnp.stack([second_d, first_d], axis=1),
        ],
        axis=1,
    )
    halves = 2 if row_count % (2 * lax.axis_size("row")) == 0 else 1
    part = row_count // halves
    slabs = [
        lax.all_to_all(hopping[:, :, h * part : (h + 1) * part], "row", 2, 1, tiled=True)
        for h in range(halves)
    ]
    tiles = []
    for slab in slabs:
        blocks = jnp.einsum("kmpr,prac->kmac", coef, slab, precision=lax.Precision.HIGHEST)
        tiles.append(lax.all_to_all(blocks, "row", 0, 2, tiled=True))
    pieces = 0.0
    for h, tile in enumerate(tiles):
        rows = state_rows[..., h * part : (h + 1) * part]
        pieces = pieces + project(tile[:, 0::2], tile[:, 1::2], rows, states)
    totals = lax.psum(pieces, "rows")
    norm = jnp.sum(states[0] * states[0] + states[1] * states[1], axis=-1)
    return (totals[:, 0] / norm, totals[:, 1] / norm)


def solution(mesh):
    placed = (P(None, "row", "rows", None), P(), P(), P(), P(None, "row", None, None))
    return jax.shard_map(
        per_device,
        mesh=mesh,
        in_specs=placed,
        out_specs=(P("row", None), P("row", None)),
        check_vma=False,
    )
```

profile of v0, /device:TPU:0, one launch (start us, length us, event | category | flops | bytes accessed | tf_op | source)
XLA Modules:
  0.0 336.3 jit_solution(9086962714207219015)
XLA Ops:
  0.6 6.6 %fusion.61 = (f32[2,8,128,512]{3,2,1,0:T(8,128)S(1)}, f32[2,8,128,512]{3,2,1,0:T(8,128)}) fusion(f32[2,8,256,512]{3,2,1,0:T(8,128)} %param.5), kind=kLoop, calls=%fused_computation.77 | loop fusion | bytes 16777216 | tf_op jit(solution)/shard_map/slice | solution.py:49
  7.2 4.4 %copy.48 = f32[2,8,128,512]{3,1,0,2:T(8,128)} copy(f32[2,8,128,512]{3,2,1,0:T(8,128)S(1)} %get-tuple-element.8) | data formatting | bytes 8388608
  11.6 7.5 %all-to-all-start.2 = ((f32[2,8,128,512]{3,1,0,2:T(8,128)}), f32[2,8,128,512]{3,1,0,2:T(8,128)}, u32[]{:S(2)}, u32[]{:S(2)}) async-start(f32[2,8,128,512]{3,1,0,2:T(8,128)} %copy.48), calls=%async_computation.2 | async-start | bytes 8388608 | tf_op jit(solution)/shard_map/all_to_all | solution.py:49
  19.1 6.6 %copy.47 = f32[2,8,128,512]{3,1,0,2:T(8,128)} copy(f32[2,8,128,512]{3,2,1,0:T(8,128)} %get-tuple-element.9) | data formatting | bytes 8388608
  25.6 0.0 copy-start.8
  25.6 0.0 copy-start.9
  25.7 0.0 copy-start.10
  25.7 71.0 %all-to-all-done.2 = f32[2,8,128,512]{3,1,0,2:T(8,128)} async-done(((f32[2,8,128,512]{3,1,0,2:T(8,128)}), f32[2,8,128,512]{3,1,0,2:T(8,128)}, u32[]{:S(2)}, u32[]{:S(2)}) %all-to-all-start.2) | async-done | bytes 4194336 | tf_op jit(solution)/shard_map/all_to_all | solution.py:49
  96.6 19.7 %all-to-all-start = ((f32[2,8,128,512]{3,1,0,2:T(8,128)}), f32[2,8,128,512]{3,1,0,2:T(8,128)}, u32[]{:S(2)}, u32[]{:S(2)}) async-start(f32[2,8,128,512]{3,1,0,2:T(8,128)} %copy.47), calls=%async_computation | async-start | bytes 8388608 | tf_op jit(solution)/shard_map/all_to_all | solution.py:49
  116.3 0.0 copy-done.8
  116.3 0.0 copy-done.9
  116.4 0.1 multiply_reduce_fusion.1
  116.4 0.0 copy-done.10
  116.4 0.1 multiply_reduce_fusion
  116.5 0.1 fusion.60
  116.6 4.2 %fusion.35 = f32[32,4,8,512]{3,0,2,1:T(8,128)S(1)} fusion(f32[2,8,16,8,512]{4,1,0,3,2:T(8,128)} %bitcast.33, f32[32,1,2,128]{3,0,2,1:T(8,128)S(1)} %get-tuple-element.22, f32[32,1,2,128]{3,0,2,1:T(8,128)S(1)} %get-tuple-element.23, f32[32,1,2,128]{3,0,2,1:T(8,128)S(1)} %get-tuple-element.14, f32[32,1,2,128]{3,0,2,1:T(8,128)S(1)} %get-tuple-element.13), kind=kOutput, calls=%fused_computation.39 | convolution fusion | flops 1610711040 | bytes 6422528 | tf_op jit(solution)/shard_map/kmpr,prac->kmac/dot_general | solution.py:54
  120.8 2.6 copy.37
  123.4 70.5 %all-to-all-done = f32[2,8,128,512]{3,1,0,2:T(8,128)} async-done(((f32[2,8,128,512]{3,1,0,2:T(8,128)}), f32[2,8,128,512]{3,1,0,2:T(8,128)}, u32[]{:S(2)}, u32[]{:S(2)}) %all-to-all-start) | async-done | bytes 4194336 | tf_op jit(solution)/shard_map/all_to_all | solution.py:49
  193.9 19.6 %all-to-all-start.3 = ((f32[32,4,8,512]{3,2,1,0:T(8,128)}), f32[32,4,8,512]{3,2,1,0:T(8,128)S(1)}, u32[]{:S(2)}, u32[]{:S(2)}) async-start(f32[32,4,8,512]{3,2,1,0:T(8,128)} %copy.37), calls=%async_computation.3 | async-start | bytes 4194304 | tf_op jit(solution)/shard_map/all_to_all | solution.py:55
  213.5 4.2 %fusion.32 = f32[32,4,8,512]{3,0,2,1:T(8,128)S(1)} fusion(f32[2,8,16,8,512]{4,1,0,3,2:T(8,128)} %bitcast.10, f32[32,1,2,128]{3,0,2,1:T(8,128)S(1)} %get-tuple-element.22, f32[32,1,2,128]{3,0,2,1:T(8,128)S(1)} %get-tuple-element.23, f32[32,1,2,128]{3,0,2,1:T(8,128)S(1)} %get-tuple-element.14, f32[32,1,2,128]{3,0,2,1:T(8,128)S(1)} %get-tuple-element.13), kind=kOutput, calls=%fused_computation.38 | convolution fusion | flops 1610711040 | bytes 6422528 | tf_op jit(solution)/shard_map/kmpr,prac->kmac/dot_general | solution.py:54
  217.7 2.6 copy.31
  220.2 34.2 %all-to-all-done.3 = f32[32,4,8,512]{3,2,1,0:T(8,128)S(1)} async-done(((f32[32,4,8,512]{3,2,1,0:T(8,128)}), f32[32,4,8,512]{3,2,1,0:T(8,128)S(1)}, u32[]{:S(2)}, u32[]{:S(2)}) %all-to-all-start.3) | async-done | bytes 2097184 | tf_op jit(solution)/shard_map/all_to_all | solution.py:55
  254.5 0.0 copy-start
  254.5 1.3 copy-done
  255.8 11.3 %all-to-all-start.1 = ((f32[32,4,8,512]{3,2,1,0:T(8,128)}), f32[32,4,8,512]{3,2,1,0:T(8,128)}, u32[]{:S(2)}, u32[]{:S(2)}) async-start(f32[32,4,8,512]{3,2,1,0:T(8,128)} %copy.31), calls=%async_computation.1 | async-start | bytes 4194304 | tf_op jit(solution)/shard_map/all_to_all | solution.py:55
  267.1 3.5 %dynamic-slice_bitcast_fusion.1 = (f32[2,128,1024]{1,2,0:T(8,128)}, f32[2,128,1024]{1,2,0:T(8,128)S(1)}, f32[2,128,1024]{1,2,0:T(8,128)S(1)}, f32[2,128,1024]{1,2,0:T(8,128)S(1)}) fusion(f32[2,2,1024,512]{3,2,1,0:T(8,128)} %param.9, s32[]{:T(128)S(6)} %add.65, s32[]{:T(128)S(6)} %add.64, s32[]{:T(128)S(6)} %select_n.37), kind=kLoop, calls=%fused_computation.41 | loop fusion | bytes 8388620 | tf_op jit(solution)/shard_map/transpose | solution.py:26
  270.6 2.5 copy.34
  273.2 1.3 copy.33
  274.5 0.3 copy.28
  274.9 1.4 copy.39
  276.2 0.0 copy-start.1
  276.2 0.0 slice-start
  276.3 4.2 %fusion.21 = f32[2,1024]{1,0:T(2,128)S(1)} fusion(f32[2,2,1024,512]{3,2,1,0:T(8,128)} %param.9), kind=kLoop, calls=%fused_computation.22 | loop fusion | flops 4192256 | bytes 8396800 | tf_op jit(solution)/shard_map/reduce_sum | solution.py:61
  280.5 0.0 copy-done.1
  280.5 0.0 slice-start.1
  280.5 0.2 copy.68
  280.7 5.6 %fusion.12 = f32[2,2,128,1024]{3,2,1,0:T(8,128)} fusion(f32[2,2,1024,512]{3,2,1,0:T(8,128)} %param.9, f32[2,4,128,512]{3,2,1,0:T(8,128)S(1)} %bitcast.135), kind=kOutput, calls=%fused_computation.12 | convolution fusion | flops 1610612736 | bytes 7340032 | tf_op jit(solution)/shard_map/kmac,kic->kmai/dot_general | solution.py:23
  286.3 0.0 slice-done
  286.3 0.0 slice-done.1
  286.3 3.5 %fusion.4 = f32[2,2,128,1024]{3,2,1,0:T(8,128)} fusion(f32[2,2,1024,512]{3,2,1,0:T(8,128)S(1)} %bitcast.132, f32[2,4,128,512]{3,2,1,0:T(8,128)S(1)} %bitcast.136), kind=kOutput, calls=%fused_computation.4 | convolution fusion | flops 1610612736 | bytes 7340032 | tf_op jit(solution)/shard_map/kmac,kic->kmai/dot_general | solution.py:23
  289.7 3.5 %fusion.6 = f32[2,2,128,1024]{3,2,1,0:T(8,128)} fusion(f32[2,2,1024,512]{3,2,1,0:T(8,128)S(1)} %bitcast.132, f32[2,4,128,512]{3,2,1,0:T(8,128)S(1)} %bitcast.137), kind=kOutput, calls=%fused_computation.6 | convolution fusion | flops 1610612736 | bytes 7340032 | tf_op jit(solution)/shard_map/kmac,kic->kmai/dot_general | solution.py:20
  293.2 14.9 %all-to-all-done.1 = f32[32,4,8,512]{3,2,1,0:T(8,128)} async-done(((f32[32,4,8,512]{3,2,1,0:T(8,128)}), f32[32,4,8,512]{3,2,1,0:T(8,128)}, u32[]{:S(2)}, u32[]{:S(2)}) %all-to-all-start.1) | async-done | bytes 2097184 | tf_op jit(solution)/shard_map/all_to_all | solution.py:55
  308.1 1.9 copy.69
  310.1 0.0 slice-start.3
  310.1 4.3 %fusion.16 = f32[2,2,128,1024]{3,2,1,0:T(8,128)S(1)} fusion(f32[2,2,1024,512]{3,2,1,0:T(8,128)} %param.9, f32[2,4,128,512]{3,2,1,0:T(8,128)S(1)} %bitcast.139), kind=kOutput, calls=%fused_computation.16 | convolution fusion | flops 1610612736 | bytes 7340032 | tf_op jit(solution)/shard_map/kmac,kic->kmai/dot_general | solution.py:23
  314.3 0.0 copy-start.7
  314.4 4.4 %fusion.8 = f32[2,2,128,1024]{3,2,1,0:T(8,128)S(1)} fusion(f32[2,2,1024,512]{3,2,1,0:T(8,128)} %param.9, f32[2,4,128,512]{3,2,1,0:T(8,128)S(1)} %bitcast.140), kind=kOutput, calls=%fused_computation.8 | convolution fusion | flops 1610612736 | bytes 7340032 | tf_op jit(solution)/shard_map/kmac,kic->kmai/dot_general | solution.py:23
  318.8 0.0 slice-done.2
  318.8 0.0 slice-done.3
  318.8 0.0 copy-start.2
  318.8 0.0 copy-start.3
  318.8 0.0 copy-start.4
  318.9 0.0 copy-start.6
  318.9 2.2 fusion.10
  321.1 0.0 copy-done.7
  321.1 0.0 copy-done.2
  321.1 0.0 copy-done.3
  321.1 0.6 copy-done.4
  321.7 0.2 copy-done.6
  321.9 2.7 add_reduce_fusion
  324.7 0.0 copy-done.5
  324.7 2.7 add_reduce_fusion.1
  327.4 8.2 %psum.7 = f32[2,2,1024]{2,1,0:T(2,128)S(1)} all-reduce(f32[2,2,1024]{2,1,0:T(2,128)S(1)} %add.62), channel_id=1, replica_groups=mesh['row'=16,'rows'=2] {'rows'}, use_global_device_ids=true, to_apply=%region_4.5 | all-reduce | flops 4096 | bytes 32768 | tf_op jit(solution)/shard_map/psum | solution.py:60
  335.7 0.6 bitcast_divide_fusion
  (8 shorter events, 0.0 us)
Async XLA Ops:
  11.6 85.0 %all-to-all-start.2 = ((f32[2,8,128,512]{3,1,0,2:T(8,128)}), f32[2,8,128,512]{3,1,0,2:T(8,128)}, u32[]{:S(2)}, u32[]{:S(2)}) async-start(f32[2,8,128,512]{3,1,0,2:T(8,128)} %copy.48), calls=%async_computation.2 | async-start | bytes 8388608 | tf_op jit(solution)/shard_map/all_to_all | solution.py:49
  25.6 90.7 %copy-start.8 = (s32[3,128]{1,0:T(4,128)S(1)}, s32[3,128]{1,0:T(4,128)}, u32[]{:S(2)}) copy-start(s32[3,128]{1,0:T(4,128)} %param.6) | copy-start | bytes 4612
  25.6 90.7 %copy-start.9 = (s32[3,32]{1,0:T(4,128)S(1)}, s32[3,32]{1,0:T(4,128)}, u32[]{:S(2)}) copy-start(s32[3,32]{1,0:T(4,128)} %param.7) | copy-start | bytes 1156
  25.7 90.8 %copy-start.10 = (f32[3,32]{1,0:T(4,128)S(1)}, f32[3,32]{1,0:T(4,128)}, u32[]{:S(2)}) copy-start(f32[3,32]{1,0:T(4,128)} %param.8) | copy-start | bytes 1156
  96.6 97.2 %all-to-all-start = ((f32[2,8,128,512]{3,1,0,2:T(8,128)}), f32[2,8,128,512]{3,1,0,2:T(8,128)}, u32[]{:S(2)}, u32[]{:S(2)}) async-start(f32[2,8,128,512]{3,1,0,2:T(8,128)} %copy.47), calls=%async_computation | async-start | bytes 8388608 | tf_op jit(solution)/shard_map/all_to_all | solution.py:49
  193.9 60.6 %all-to-all-start.3 = ((f32[32,4,8,512]{3,2,1,0:T(8,128)}), f32[32,4,8,512]{3,2,1,0:T(8,128)S(1)}, u32[]{:S(2)}, u32[]{:S(2)}) async-start(f32[32,4,8,512]{3,2,1,0:T(8,128)} %copy.37), calls=%async_computation.3 | async-start | bytes 4194304 | tf_op jit(solution)/shard_map/all_to_all | solution.py:55
  254.5 1.3 copy-start
  255.8 52.3 %all-to-all-start.1 = ((f32[32,4,8,512]{3,2,1,0:T(8,128)}), f32[32,4,8,512]{3,2,1,0:T(8,128)}, u32[]{:S(2)}, u32[]{:S(2)}) async-start(f32[32,4,8,512]{3,2,1,0:T(8,128)} %copy.31), calls=%async_computation.1 | async-start | bytes 4194304 | tf_op jit(solution)/shard_map/all_to_all | solution.py:55
  276.2 4.2 %copy-start.1 = (f32[32,4,8,512]{3,2,1,0:T(8,128)S(1)}, f32[32,4,8,512]{3,2,1,0:T(8,128)}, u32[]{:S(2)}) copy-start(f32[32,4,8,512]{3,2,1,0:T(8,128)} %copy-done) | copy-start | bytes 6291460
  276.2 10.0 %slice-start = ((s8[8388608]{0:T(1024)(128)(4,1)}), s8[4194304]{0:T(1024)(128)(4,1)S(1)}, s32[]{:S(2)}) async-start(s8[8388608]{0:T(1024)(128)(4,1)} %bitcast.131), calls=%async_computation.4 | async-start | bytes 8388608
  280.5 5.8 %slice-start.1 = ((s8[8388608]{0:T(1024)(128)(4,1)}), s8[4194304]{0:T(1024)(128)(4,1)S(1)}, s32[]{:S(2)}) async-start(s8[8388608]{0:T(1024)(128)(4,1)} %bitcast.131), calls=%async_computation.5 | async-start | bytes 8388608
  308.1 10.7 %slice-start.2 = ((s8[8388608]{0:T(1024)(128)(4,1)}), s8[4194304]{0:T(1024)(128)(4,1)S(1)}, s32[]{:S(2)}) async-start(s8[8388608]{0:T(1024)(128)(4,1)} %bitcast.133), calls=%async_computation.6 | async-start | bytes 8388608
  310.1 8.7 %slice-start.3 = ((s8[8388608]{0:T(1024)(128)(4,1)}), s8[4194304]{0:T(1024)(128)(4,1)S(1)}, s32[]{:S(2)}) async-start(s8[8388608]{0:T(1024)(128)(4,1)} %bitcast.133), calls=%async_computation.7 | async-start | bytes 8388608
  314.3 6.7 %copy-start.7 = (f32[2,128,1024]{2,1,0:T(8,128)S(1)}, f32[2,128,1024]{2,1,0:T(8,128)}, u32[]{:S(2)}) copy-start(f32[2,128,1024]{2,1,0:T(8,128)} %copy.39) | copy-start | bytes 3145732
  318.8 2.2 copy-start.2
  318.8 2.2 copy-start.3
  318.8 2.8 copy-start.4
  318.9 3.1 copy-start.6
  321.9 2.7 copy-start.5
where the time goes:
time: 342 us; the launch traced here: 336 us
  waiting for transfers between devices  191 us (56%)
  starting transfers between devices  58.1 us (17%)
  matrix products  37.2 us (11%)
  local copies, waits for them, and re-layouts  36.2 us (11%)
  blocking collectives  8.23 us (2%)
  other arithmetic  5.11 us (1%)
    all_to_all x2, waiting for transfers between devices, per_device(): lax.all_to_all(hopping[:, :, h * part:(h + 1) * part], 'row', 2, 1, tiled...  141 us
    all_to_all x2, waiting for transfers between devices, per_device(): tiles.append(lax.all_to_all(blocks, 'row', 0, 2, tiled=True))  49.1 us
    all_to_all x2, starting transfers between devices, per_device(): tiles.append(lax.all_to_all(blocks, 'row', 0, 2, tiled=True))  30.9 us
    all_to_all x2, starting transfers between devices, per_device(): lax.all_to_all(hopping[:, :, h * part:(h + 1) * part], 'row', 2, 1, tiled...  27.2 us
    unnamed x32, local copies, waits for them, and re-layouts  13.2 us
    dot_general x2, matrix products, project(): jnp.einsum('kmac,kic->kmai', m_re, cols[1], precision=high)  9.83 us
    dot_general x2, matrix products, per_device(): jnp.einsum('kmpr,prac->kmac', coef, slab, precision=lax.Precision.HIGHEST)  8.33 us
    psum x1, blocking collectives, per_device(): totals = lax.psum(pieces, 'rows')  8.23 us
  transfers between devices with their start and end apart: 4, of which 4 were waited for; matrix products, arithmetic and copies ran while one was open for 14% of the time, Pallas kernels for 0%

commit v1 on v0

--- a/solution.py
+++ b/solution.py
@@ -1,11 +1,20 @@
+import functools
 import math
 
 import jax
 import jax.numpy as jnp
 from jax import lax
+from jax.experimental import pallas as pl
+from jax.experimental.pallas import tpu as pltpu
 from jax.sharding import PartitionSpec as P
 
 KGRID = 8
+LINE = 4
+LANES = 128
+SUB = 16
+MESH = pl.DeviceIdType.MESH
+F32 = jnp.float32
+BF16 = jnp.bfloat16
 
 
 def phases(kgrid, lattice, tangent):
@@ -13,6 +22,488 @@
     angle = turns.astype(jnp.float32) * (2.0 * math.pi / KGRID)
     weight = jnp.sum(tangent[:, :, None] * lattice[:, None, :].astype(jnp.float32), axis=0)
     return (jnp.cos(angle), jnp.sin(angle), weight)
+
+
+def split(value):
+    high = value.astype(BF16)
+    return high, (value - high.astype(F32)).astype(BF16)
+
+
+def coefficients(lattice, kgrid, tangent, group, per):
+    place = lax.axis_index("row") // group
+    count = group * per
+    mine = lax.dynamic_slice_in_dim(lattice, place * count, count, 1)
+    cosine, sine, weight = (v.reshape(-1, group, 1, per) for v in phases(kgrid, mine, tangent))
+    plus, minus = 0.5 * (cosine + sine), 0.5 * (cosine - sine)
+    energy = jnp.concatenate([plus, minus], axis=2)
+    slope = weight * jnp.concatenate([minus, -plus], axis=2)
+    coef = jnp.stack([energy, slope], axis=1)
+    coef = coef.reshape(LINE, -1, 2 * count)
+    coef = jnp.where(place < LINE // 2, coef, coef[::-1])
+    return coef.reshape(-1, 2 * count)
+
+
+def kernel(
+    dims,
+    coef_ref,
+    hop,
+    states,
+    energy_ref,
+    slope_ref,
+    coef3,
+    hown,
+    ht,
+    uvs,
+    uva,
+    part,
+    got1,
+    got2,
+    tk,
+    st,
+    wide,
+    fine,
+    acc,
+    sums,
+    hsem,
+    tsem,
+    ssem,
+    xs,
+    xr,
+    gs,
+    gr,
+    s1,
+    r1,
+    s2,
+    r2,
+    s3,
+    r3,
+    ds,
+    dr,
+    es,
+    er,
+):
+    X, G, per, nb, kd, NB = dims
+    nbc = nb // LANES
+    nch = X * nbc
+    span = G * SUB
+    nsub = nb // span
+    nt = nch * nsub
+    kb = part.shape[2]
+    slots = st.shape[0]
+    row, x = lax.axis_index("row"), lax.axis_index("rows")
+    a, g = row // G, lax.rem(row, G)
+    outer = (a == 0) | (a == LINE - 1)
+    inner = jnp.logical_not(outer)
+    beside = a + 1 - 2 * lax.rem(a, 2)
+    across = LINE - 1 - a
+    own = jnp.where(outer, 0, 1)
+
+    def column(j):
+        home = lax.rem(x + j // nbc, X)
+        return pl.multiple_of(home * nb + lax.rem(j, nbc) * LANES, LANES)
+
+    def at(position, member):
+        return {"row": position * G + member, "rows": x}
+
+    def remote(src, dst, send, recv, device):
+        return pltpu.make_async_remote_copy(
+            src_ref=src, dst_ref=dst, send_sem=send, recv_sem=recv, device_id=device, device_id_type=MESH
+        )
+
+    def load_own(j):
+        slot = lax.rem(j, 2)
+        return pltpu.make_async_copy(hop.at[:, :, :, pl.ds(column(j), LANES)], hown.at[slot], hsem.at[slot])
+
+    def load_turned(j):
+        start = pl.multiple_of(x * nb, LANES)
+        return pltpu.make_async_copy(
+            hop.at[:, :, pl.ds(j * LANES, LANES), pl.ds(start, nb)], ht.at[j], tsem.at[j]
+        )
+
+    def load_states(j):
+        slot = lax.rem(j, slots)
+        return pltpu.make_async_copy(states.at[:, :, :, pl.ds(column(j), LANES)], st.at[slot], ssem.at[slot])
+
+    def turned_copy(o, q):
+        to = lax.rem(x - o + X, X)
+        start = pl.multiple_of(to * nb, LANES)
+        n = (o - 1) * nbc + q
+        return remote(
+            hop.at[:, :, pl.ds(q * LANES, LANES), pl.ds(start, nb)],
+            ht.at[o * nbc + q],
+            xs.at[n],
+            xr.at[n],
+            {"row": row, "rows": to},
+        )
+
+    def turned_arrival(j):
+        return remote(ht.at[j], ht.at[j], xs.at[j - nbc], xr.at[j - nbc], {"row": row, "rows": lax.rem(x + 1, X)})
+
+    def share_copy(t, o):
+        to = lax.rem(g + o, G)
+        return remote(uvs.at[t, to], uva.at[t, g], gs.at[t, o - 1], gr.at[t, o - 1], at(a, to))
+
+    def share_arrival(t, o):
+        source = lax.rem(g - o + G, G)
+        return remote(uvs.at[t, source], uva.at[t, source], gs.at[t, o - 1], gr.at[t, o - 1], at(a, source))
+
+    def first_copy(t):
+        return remote(part.at[t, pl.ds(1, 3)], got1.at[t], s1.at[t], r1.at[t], at(beside, g))
+
+    def second_copy(t):
+        return remote(part.at[t, pl.ds(2, 2)], got2.at[t], s2.at[t], r2.at[t], at(across, g))
+
+    def third_copy(t):
+        return remote(part.at[t, 0], got1.at[t, 0], s3.at[t], r3.at[t], at(beside, g))
+
+    def place_of(t, member):
+        return pl.multiple_of(lax.rem(t, nsub) * span + member * SUB, SUB)
+
+    def deal_copy(t, o):
+        to = lax.rem(g + o, G)
+        return remote(
+            part.at[t, own, pl.ds(to * 2 * kd, 2 * kd)],
+            tk.at[t // nsub, :, pl.ds(place_of(t, g), SUB), :],
+            ds.at[t, o - 1],
+            dr.at[t, o - 1],
+            at(a, to),
+        )
+
+    def deal_arrival(t, o):
+        source = lax.rem(g - o + G, G)
+        there = tk.at[t // nsub, :, pl.ds(place_of(t, source), SUB), :]
+        return remote(there, there, ds.at[t, o - 1], dr.at[t, o - 1], at(a, source))
+
+    for j in range(nbc):
+        load_turned(j).start()
+    for j in range(2):
+        load_own(j).start()
+    for j in range(slots):
+        load_states(j).start()
+
+    barrier = pltpu.get_barrier_semaphore()
+    for o in range(1, X):
+        pl.semaphore_signal(barrier, inc=1, device_id={"row": row, "rows": lax.rem(x + o, X)}, device_id_type=MESH)
+    for o in range(1, G):
+        pl.semaphore_signal(barrier, inc=1, device_id=at(a, lax.rem(g + o, G)), device_id_type=MESH)
+    for o in range(1, LINE):
+        pl.semaphore_signal(barrier, inc=1, device_id=at(lax.rem(a + o, LINE), g), device_id_type=MESH)
+    pl.semaphore_wait(barrier, X + G + LINE - 3)
+
+    for q in range(nbc):
+        for o in range(1, X):
+            turned_copy(o, q).start()
+
+    high, low = split(coef_ref[...])
+    coef3[...] = jnp.concatenate([high, high, low], axis=1)
+
+    def produce(j):
+        slot = lax.rem(j, 2)
+        load_own(j).wait()
+
+        def one(r, carry):
+            for h in range(nbc):
+                rows = pl.ds(h * LANES, LANES)
+                u = hown[slot, 0, r, rows, :] - ht[j, 1, r, :, rows].T
+                v = ht[j, 0, r, :, rows].T + hown[slot, 1, r, rows, :]
+                for q in range(LANES // SUB):
+                    start = h * LANES + q * SUB
+                    t, member = j * nsub + start // span, start % span // SUB
+                    uvs[t, member, r] = u[q * SUB : (q + 1) * SUB]
+                    uvs[t, member, per + r] = v[q * SUB : (q + 1) * SUB]
+            return carry
+
+        lax.fori_loop(0, per, one, 0)
+
+        def send(s, carry):
+            t = j * nsub + s
+            for o in range(1, G):
+                share_copy(t, o).start()
+            uva[t, g] = uvs[t, g]
+            return carry
+
+        lax.fori_loop(0, nsub, send, 0)
+
+    def reload(j):
+        @pl.when(j < nch)
+        def _():
+            load_own(j).start()
+
+    def expand(t):
+        for o in range(1, G):
+            share_arrival(t, o).wait_recv()
+        for h in range(SUB // 8):
+            rows = pl.ds(h * 8, 8)
+            data = uva[t, :, :, rows, :].reshape(G * 2 * per, 8, LANES)
+            data = jnp.swapaxes(data, 0, 1)
+            done = []
+            for i in range(0, 8, 2):
+                high, low = split(jnp.concatenate([data[i], data[i + 1]], axis=1))
+                both = jnp.concatenate([high, low, high], axis=0)
+                out = jnp.dot(coef3[...], both, preferred_element_type=F32)
+                done += [out[:, :LANES], out[:, LANES:]]
+            done = jnp.swapaxes(jnp.stack(done), 0, 1)
+            part[t, :, :, rows, :] = done.reshape(LINE, kb, 8, LANES)
+
+        @pl.when(outer)
+        def _():
+            first_copy(t).start()
+
+    def deal(t):
+        for o in range(1, G):
+            deal_copy(t, o).start()
+        tk[t // nsub, :, pl.ds(place_of(t, g), SUB), :] = part[t, own, pl.ds(g * 2 * kd, 2 * kd)]
+
+    def join_first(t):
+        first_copy(t).wait_recv()
+        part[t, 1:4] += got1[t]
+        second_copy(t).start()
+
+    def join_second(t):
+        second_copy(t).wait_recv()
+        part[t, 0] += got2[t, 1]
+        third_copy(t).start()
+        part[t, 1] += got2[t, 0]
+        deal(t)
+
+    def join_third(t):
+        third_copy(t).wait_recv()
+        part[t, 0] += got1[t, 0]
+        deal(t)
+
+    def project(j):
+        def arrived(s, carry):
+            for o in range(1, G):
+                deal_arrival(j * nsub + s, o).wait_recv()
+            return carry
+
+        lax.fori_loop(0, nsub, arrived, 0)
+        slot = lax.rem(j, slots)
+
+        @pl.when(j >= slots)
+        def _():
+            load_states(j).wait()
+
+        rows_at_once = 256
+        for k in range(kd):
+            high, low = split(jnp.concatenate([tk[j, 2 * k], tk[j, 2 * k + 1]], axis=1))
+
+            def bands(b, carry):
+                rows = pl.ds(pl.multiple_of(b * rows_at_once, rows_at_once), rows_at_once)
+
+                def times(side):
+                    big, small = wide[k, side, rows, :], fine[k, side, rows, :]
+                    return (
+                        jnp.dot(big, high, preferred_element_type=F32)
+                        + jnp.dot(big, low, preferred_element_type=F32)
+                        + jnp.dot(small, high, preferred_element_type=F32)
+                    )
+
+                left, right = st[slot, 0, k, rows, :], st[slot, 1, k, rows, :]
+                minus, plus = left - right, left + right
+                over, under = times(0), times(1)
+                acc[k, 0, rows, :] += over[:, :LANES] * minus + under[:, :LANES] * plus
+                acc[k, 1, rows, :] += over[:, LANES:] * minus + under[:, LANES:] * plus
+                return carry
+
+            lax.fori_loop(0, NB // rows_at_once, bands, 0)
+
+        @pl.when(j + slots < nch)
+        def _():
+            load_states(j + slots).start()
+
+    def to_row(value):
+        return jnp.sum(value.T, axis=0, keepdims=True)
+
+    def prepare():
+        for j in range(slots):
+            load_states(j).wait()
+        for k in range(kd):
+
+            def bands(b, carry):
+                rows = pl.ds(pl.multiple_of(b * LANES, LANES), LANES)
+                total = jnp.zeros((LANES, LANES), F32)
+                for q in range(nbc):
+                    for side in range(2):
+                        value = st[q, side, k, rows, :]
+                        high, low = split(value)
+                        wide[k, side, rows, q * LANES : (q + 1) * LANES] = high
+                        fine[k, side, rows, q * LANES : (q + 1) * LANES] = low
+                        total = total + value * value
+                acc[k, 0, rows, :] = jnp.zeros((LANES, LANES), F32)
+                acc[k, 1, rows, :] = jnp.zeros((LANES, LANES), F32)
+                sums[x, pl.ds(2 * kd + k, 1), rows] = to_row(total)
+                return carry
+
+            lax.fori_loop(0, NB // LANES, bands, 0)
+
+    for j in range(nbc):
+        load_turned(j).wait()
+        produce(j)
+        reload(j + 2)
+    prepare()
+
+    lag = 5
+
+    def step(t, carry):
+        @pl.when(t < nt)
+        def _():
+            expand(t)
+
+        @pl.when(inner & (t >= 1) & (t - 1 < nt))
+        def _():
+            join_first(t - 1)
+
+        @pl.when(inner & (t >= 2) & (t - 2 < nt))
+        def _():
+            join_second(t - 2)
+
+        @pl.when(outer & (t >= 4) & (t - 4 < nt))
+        def _():
+            join_third(t - 4)
+
+        j = t // nsub + 1
+
+        @pl.when((lax.rem(t, nsub) == nsub - 1) & (j >= nbc) & (j < nch))
+        def _():
+            turned_arrival(j).wait_recv()
+            produce(j)
+            reload(j + 2)
+
+        done = t - lag
+
+        @pl.when((done >= 0) & (lax.rem(done + nsub, nsub) == nsub - 1))
+        def _():
+            project(done // nsub)
+
+        return carry
+
+    lax.fori_loop(0, nt + lag, step, 0)
+
+    for k in range(kd):
+        for m in range(2):
+
+            def bands(b, carry):
+                rows = pl.ds(pl.multiple_of(b * LANES, LANES), LANES)
+                sums[x, pl.ds(2 * k + m, 1), rows] = to_row(acc[k, m, rows, :])
+                return carry
+
+            lax.fori_loop(0, NB // LANES, bands, 0)
+
+    def sum_copy(o):
+        to = lax.rem(x + o, X)
+        return remote(sums.at[x], sums.at[x], es.at[o - 1], er.at[o - 1], {"row": row, "rows": to})
+
+    def sum_arrival(o):
+        source = lax.rem(x - o + X, X)
+        return remote(sums.at[source], sums.at[source], es.at[o - 1], er.at[o - 1], {"row": row, "rows": source})
+
+    for o in range(1, X):
+        sum_copy(o).start()
+    for o in range(1, X):
+        sum_arrival(o).wait_recv()
+    total = sums[0]
+    for o in range(1, X):
+        total = total + sums[o]
+    for k in range(kd):
+        norm = total[2 * kd + k : 2 * kd + k + 1]
+        energy_ref[k : k + 1, :] = total[2 * k : 2 * k + 1] / norm
+        slope_ref[k : k + 1, :] = total[2 * k + 1 : 2 * k + 2] / norm
+
+    for q in range(nbc):
+        for o in range(1, X):
+            turned_copy(o, q).wait_send()
+    for o in range(1, X):
+        sum_copy(o).wait_send()
+
+    def settle(t, carry):
+        for o in range(1, G):
+            share_copy(t, o).wait_send()
+            deal_copy(t, o).wait_send()
+
+        @pl.when(outer)
+        def _():
+            first_copy(t).wait_send()
+
+        @pl.when(inner)
+        def _():
+            second_copy(t).wait_send()
+            third_copy(t).wait_send()
+
+        return carry
+
+    lax.fori_loop(0, nt, settle, 0)
+
+
+def fits(row, X, hopping, states):
+    per, nb, columns = hopping.shape[1:]
+    kd, bands = states.shape[1:3]
+    if row % LINE or nb % LANES or X < 2 or columns != X * nb:
+        return False
+    group = row // LINE
+    nbc, span = nb // LANES, group * SUB
+    return group > 1 and nbc >= 2 and nb % span == 0 and (span <= LANES or span % LANES == 0) and bands % 256 == 0
+
+
+def one_kernel(hopping, lattice, kgrid, tangent, states):
+    X, G = lax.axis_size("rows"), lax.axis_size("row") // LINE
+    per, nb = hopping.shape[1:3]
+    kd, NB = states.shape[1:3]
+    nbc = nb // LANES
+    nch = X * nbc
+    nt = nch * nb // (G * SUB)
+    coef = coefficients(lattice, kgrid, tangent, G, per)
+    kb = coef.shape[0] // LINE
+    cols = coef.shape[1]
+    slots = nbc
+    tile = (SUB, LANES)
+    dma = pltpu.SemaphoreType.DMA
+    out = jax.ShapeDtypeStruct((kd, NB), F32)
+    vmem = pl.BlockSpec(memory_space=pltpu.VMEM)
+    hbm = pl.BlockSpec(memory_space=pl.ANY)
+    rows_of_sums = -(-3 * kd // 8) * 8
+    return pl.pallas_call(
+        functools.partial(kernel, (X, G, per, nb, kd, NB)),
+        out_shape=(out, out),
+        in_specs=[vmem, hbm, hbm],
+        out_specs=(vmem, vmem),
+        scratch_shapes=[
+            pltpu.VMEM((LINE * kb, 3 * cols), BF16),
+            pltpu.VMEM((2, 2, per, nb, LANES), F32),
+            pltpu.VMEM((nch, 2, per, LANES, nb), F32),
+            pltpu.VMEM((nt, G, 2 * per, *tile), F32),
+            pltpu.VMEM((nt, G, 2 * per, *tile), F32),
+            pltpu.VMEM((nt, LINE, kb, *tile), F32),
+            pltpu.VMEM((nt, LINE - 1, kb, *tile), F32),
+            pltpu.VMEM((nt, LINE // 2, kb, *tile), F32),
+            pltpu.VMEM((nch, 2 * kd, nb, LANES), F32),
+            pltpu.VMEM((slots, 2, kd, NB, LANES), F32),
+            pltpu.VMEM((kd, 2, NB, nb), BF16),
+            pltpu.VMEM((kd, 2, NB, nb), BF16),
+            pltpu.VMEM((kd, 2, NB, LANES), F32),
+            pltpu.VMEM((X, rows_of_sums, NB), F32),
+            dma((2,)),
+            dma((nbc,)),
+            dma((slots,)),
+            dma(((X - 1) * nbc,)),
+            dma(((X - 1) * nbc,)),
+            dma((nt, G - 1)),
+            dma((nt, G - 1)),
+            dma((nt,)),
+            dma((nt,)),
+            dma((nt,)),
+            dma((nt,)),
+            dma((nt,)),
+            dma((nt,)),
+            dma((nt, G - 1)),
+            dma((nt, G - 1)),
+            dma((X - 1,)),
+            dma((X - 1,)),
+        ],
+        compiler_params=pltpu.CompilerParams(
+            collective_id=0, has_side_effects=True, vmem_limit_bytes=67043328
+        ),
+    )(coef, hopping, states)
 
 
 def project(m_re, m_im, rows, cols):
@@ -28,7 +519,7 @@
     return jnp.sum(a * y_re + b * y_im, axis=2)
 
 
-def per_device(hopping, lattice, kgrid, tangent, states):
+def exchanges(hopping, lattice, kgrid, tangent, states):
     row_count = hopping.shape[2]
     row_start = lax.axis_index("rows") * row_count
     state_rows = lax.dynamic_slice_in_dim(states, row_start, row_count, 3)
@@ -62,6 +553,12 @@
     return (totals[:, 0] / norm, totals[:, 1] / norm)
 
 
+def per_device(hopping, lattice, kgrid, tangent, states):
+    if fits(lax.axis_size("row"), lax.axis_size("rows"), hopping, states):
+        return one_kernel(hopping, lattice, kgrid, tangent, states)
+    return exchanges(hopping, lattice, kgrid, tangent, states)
+
+
 def solution(mesh):
     placed = (P(None, "row", "rows", None), P(), P(), P(), P(None, "row", None, None))
     return jax.shard_map(

time: 342 us -> 184 us (0.54); the launches traced: 336 us -> 184 us
  waiting for transfers between devices: 191 us -> 0 us
  Pallas kernels: 0 us -> 177 us
  starting transfers between devices: 58.1 us -> 0 us
  matrix products: 37.2 us -> 0 us
  local copies, waits for them, and re-layouts: 36.2 us -> 3.27 us
  blocking collectives: 8.23 us -> 0 us
    all_to_all x4 -> x0, waiting for transfers between devices: 191 us -> none  [the longest x2 141 us: per_device(): lax.all_to_all(hopping[:, :, h * part:(h + 1) * part], 'row', 2, 1, tiled...]
    pallas_call x0 -> x1, Pallas kernels: none -> 177 us  [one_kernel(): pl.pallas_call(functools.partial(kernel, (X, G, per, nb, kd, NB)), out_sh...]
    all_to_all x4 -> x0, starting transfers between devices: 58.1 us -> none  [the longest x2 30.9 us: per_device(): tiles.append(lax.all_to_all(blocks, 'row', 0, 2, tiled=True))]
    dot_general x10 -> x0, matrix products: 37.2 us -> none  [the longest x2 9.83 us: project(): jnp.einsum('kmac,kic->kmai', m_re, cols[1], precision=high)]
    unnamed x32 -> x2, local copies, waits for them, and re-layouts: 13.2 us -> 2.59 us
    transpose x5 -> x0, local copies, waits for them, and re-layouts: 9.13 us -> none  [the longest x3 6.41 us: project(): a = jnp.swapaxes(rows[0], 1, 2)[:, None]]
    psum x1 -> x0, blocking collectives: 8.23 us -> none  [per_device(): totals = lax.psum(pieces, 'rows')]
    slice x2 -> x0, local copies, waits for them, and re-layouts: 6.64 us -> none  [the longest x1 6.62 us: per_device(): hopping[:, :, h * part:(h + 1) * part]]
  transfers between devices with their start and end apart: 4 -> 0, of which waited for: 4 -> 0; matrix products, arithmetic and copies ran while one was open for 14% -> 0% of each run, Pallas kernels for 0% -> 0%
where the time goes in v1:
time: 184 us
  Pallas kernels  177 us (96%)
  local copies, waits for them, and re-layouts  3.27 us (2%)
  other arithmetic  3.01 us (2%)
    pallas_call x1, Pallas kernels, one_kernel(): pl.pallas_call(functools.partial(kernel, (X, G, per, nb, kd, NB)), out_sh...  177 us

profile of v1, /device:TPU:0, one launch (start us, length us, event | category | flops | bytes accessed | tf_op | source)
XLA Modules:
  0.0 183.7 jit_solution(1083674714328420938)
XLA Ops:
  0.7 0.8 fusion.6
  1.4 0.8 multiply_reduce_fusion
  2.2 0.1 copy.11
  2.2 0.8 multiply_reduce_fusion.1
  3.0 0.1 copy.10
  3.1 0.1 add_multiply_fusion
  3.2 0.2 copy.12
  3.5 0.3 reshape.187
  3.8 0.6 reverse_select_fusion
  4.4 176.7 %shard_map.68 = (f32[2,1024]{1,0:T(2,128)}, f32[2,1024]{1,0:T(2,128)}) custom-call(f32[64,64]{1,0:T(8,128)} %bitcast.28, f32[2,8,256,512]{3,2,1,0:T(8,128)} %hop.1, f32[2,2,1024,512]{3,2,1,0:T(8,128)} %states.1), custom_call_target="tpu_custom_call" | custom-call | tf_op jit(solution)/shard_map/pallas_call | solution.py:465
  181.1 1.3 copy.15
  182.4 1.3 copy.16
  (3 shorter events, 0.0 us)

commit v2 on v1

--- a/solution.py
+++ b/solution.py
@@ -9,47 +9,73 @@
 from jax.sharding import PartitionSpec as P
 
 KGRID = 8
+AHEAD = 2
+FLIGHT = 2
+LAGS = (1, 3, 8)
+SHIFT = 1
 LINE = 4
 LANES = 128
-SUB = 16
+SUB = 8
 MESH = pl.DeviceIdType.MESH
 F32 = jnp.float32
 BF16 = jnp.bfloat16
 
 
-def phases(kgrid, lattice, tangent):
-    turns = jnp.mod(jnp.sum(kgrid[:, :, None] * lattice[:, None, :], axis=0), KGRID)
-    angle = turns.astype(jnp.float32) * (2.0 * math.pi / KGRID)
-    weight = jnp.sum(tangent[:, :, None] * lattice[:, None, :].astype(jnp.float32), axis=0)
-    return (jnp.cos(angle), jnp.sin(angle), weight)
-
-
 def split(value):
     high = value.astype(BF16)
     return high, (value - high.astype(F32)).astype(BF16)
 
 
-def coefficients(lattice, kgrid, tangent, group, per):
-    place = lax.axis_index("row") // group
-    count = group * per
-    mine = lax.dynamic_slice_in_dim(lattice, place * count, count, 1)
-    cosine, sine, weight = (v.reshape(-1, group, 1, per) for v in phases(kgrid, mine, tangent))
+def coefficients(lattice, kgrid, tangent, place, shape, per):
+    exact = lax.Precision.HIGHEST
+    block = shape[0] // LINE
+    count = shape[1] // 2
+
+    def iota(dims, axis):
+        return lax.broadcasted_iota(jnp.int32, dims, axis)
+
+    row = iota((shape[0], kgrid.shape[1]), 0)
+    home = lax.div(row, block)
+    home = jnp.where(place < LINE // 2, home, LINE - 1 - home)
+    which = home * (block // 2) + lax.div(lax.rem(row, block), 2)
+    pick_k = (which == iota(row.shape, 1)).astype(F32)
+    column = iota((lattice.shape[1], shape[1]), 1)
+    which = place * count + lax.div(column, 2 * per) * per + lax.rem(column, per)
+    pick_r = (which == iota(column.shape, 0)).astype(F32)
+    far = jnp.dot(lattice.astype(F32), pick_r, precision=exact, preferred_element_type=F32)
+
+    def near(value):
+        return lax.dot_general(pick_k, value, (((1,), (1,)), ((), ())), precision=exact, preferred_element_type=F32)
+
+    def inner(left):
+        return left[:, 0:1] * far[0:1] + left[:, 1:2] * far[1:2] + left[:, 2:3] * far[2:3]
+
+    turns = inner(near(kgrid.astype(F32))).astype(jnp.int32) & (KGRID - 1)
+    weight = inner(near(tangent))
+
+    def wave(turn):
+        turn = turn & (KGRID - 1)
+        turn = jnp.minimum(turn, KGRID - turn)
+        value = jnp.full(shape, -1.0, F32)
+        for step in range(KGRID // 2):
+            value = jnp.where(turn == step, F32(math.cos(2.0 * math.pi * step / KGRID)), value)
+        return value
+
+    cosine, sine = wave(turns), wave(turns - KGRID // 4)
     plus, minus = 0.5 * (cosine + sine), 0.5 * (cosine - sine)
-    energy = jnp.concatenate([plus, minus], axis=2)
-    slope = weight * jnp.concatenate([minus, -plus], axis=2)
-    coef = jnp.stack([energy, slope], axis=1)
-    coef = coef.reshape(LINE, -1, 2 * count)
-    coef = jnp.where(place < LINE // 2, coef, coef[::-1])
-    return coef.reshape(-1, 2 * count)
+    second = lax.rem(lax.div(iota(shape, 1), per), 2) == 1
+    slope = lax.rem(iota(shape, 0), 2) == 1
+    return jnp.where(slope, weight * jnp.where(second, -plus, minus), jnp.where(second, minus, plus))
 
 
 def kernel(
     dims,
-    coef_ref,
+    lattice_ref,
+    kgrid_ref,
+    tangent_ref,
     hop,
     states,
-    energy_ref,
-    slope_ref,
+    out_ref,
     coef3,
     hown,
     ht,
@@ -88,6 +114,7 @@
     span = G * SUB
     nsub = nb // span
     nt = nch * nsub
+    ahead, flight = min(AHEAD, nsub), FLIGHT
     kb = part.shape[2]
     slots = st.shape[0]
     row, x = lax.axis_index("row"), lax.axis_index("rows")
@@ -174,12 +201,8 @@
         there = tk.at[t // nsub, :, pl.ds(place_of(t, source), SUB), :]
         return remote(there, there, ds.at[t, o - 1], dr.at[t, o - 1], at(a, source))
 
-    for j in range(nbc):
-        load_turned(j).start()
-    for j in range(2):
-        load_own(j).start()
-    for j in range(slots):
-        load_states(j).start()
+    load_turned(0).start()
+    load_own(0).start()
 
     barrier = pltpu.get_barrier_semaphore()
     for o in range(1, X):
@@ -188,41 +211,43 @@
         pl.semaphore_signal(barrier, inc=1, device_id=at(a, lax.rem(g + o, G)), device_id_type=MESH)
     for o in range(1, LINE):
         pl.semaphore_signal(barrier, inc=1, device_id=at(lax.rem(a + o, LINE), g), device_id_type=MESH)
+    shape = (coef3.shape[0], coef3.shape[1] // 3)
+    high, low = split(coefficients(lattice_ref[...], kgrid_ref[...], tangent_ref[...], a, shape, per))
+    coef3[...] = jnp.concatenate([high, high, low], axis=1)
+
     pl.semaphore_wait(barrier, X + G + LINE - 3)
 
-    for q in range(nbc):
-        for o in range(1, X):
-            turned_copy(o, q).start()
-
-    high, low = split(coef_ref[...])
-    coef3[...] = jnp.concatenate([high, high, low], axis=1)
-
-    def produce(j):
+    for o in range(1, X):
+        turned_copy(o, 0).start()
+    for j in range(1, nbc):
+        load_turned(j).start()
+    load_own(1).start()
+    for j in range(slots):
+        load_states(j).start()
+
+
+    batch = LANES // span
+
+    def produce(j, h):
         slot = lax.rem(j, 2)
-        load_own(j).wait()
+        rows = pl.ds(h * LANES, LANES)
+        first = j * nsub + h * batch
 
         def one(r, carry):
-            for h in range(nbc):
-                rows = pl.ds(h * LANES, LANES)
-                u = hown[slot, 0, r, rows, :] - ht[j, 1, r, :, rows].T
-                v = ht[j, 0, r, :, rows].T + hown[slot, 1, r, rows, :]
-                for q in range(LANES // SUB):
-                    start = h * LANES + q * SUB
-                    t, member = j * nsub + start // span, start % span // SUB
-                    uvs[t, member, r] = u[q * SUB : (q + 1) * SUB]
-                    uvs[t, member, per + r] = v[q * SUB : (q + 1) * SUB]
+            u = hown[slot, 0, r, rows, :] - ht[j, 1, r, :, rows].T
+            v = ht[j, 0, r, :, rows].T + hown[slot, 1, r, rows, :]
+            for q in range(LANES // SUB):
+                t, member = first + q // G, q % G
+                uvs[t, member, r] = u[q * SUB : (q + 1) * SUB]
+                uvs[t, member, per + r] = v[q * SUB : (q + 1) * SUB]
             return carry
 
         lax.fori_loop(0, per, one, 0)
 
-        def send(s, carry):
-            t = j * nsub + s
-            for o in range(1, G):
-                share_copy(t, o).start()
-            uva[t, g] = uvs[t, g]
-            return carry
-
-        lax.fori_loop(0, nsub, send, 0)
+    def share(t):
+        for o in range(1, G):
+            share_copy(t, o).start()
+        uva[t, g] = uvs[t, g]
 
     def reload(j):
         @pl.when(j < nch)
@@ -247,6 +272,10 @@
 
         @pl.when(outer)
         def _():
+            @pl.when(t >= flight)
+            def _():
+                first_copy(t - flight).wait_send()
+
             first_copy(t).start()
 
     def deal(t):
@@ -284,7 +313,7 @@
         def _():
             load_states(j).wait()
 
-        rows_at_once = 256
+        rows_at_once = 1024
         for k in range(kd):
             high, low = split(jnp.concatenate([tk[j, 2 * k], tk[j, 2 * k + 1]], axis=1))
 
@@ -337,58 +366,87 @@
 
             lax.fori_loop(0, NB // LANES, bands, 0)
 
-    for j in range(nbc):
-        load_turned(j).wait()
-        produce(j)
-        reload(j + 2)
-    prepare()
-
-    lag = 5
+    load_turned(0).wait()
+    load_own(0).wait()
+    for h in range(nbc):
+        produce(0, h)
+        for t in range(h * batch, min(ahead, (h + 1) * batch)):
+            share(t)
+    reload(2)
+
+    lag1, lag2, lag3 = LAGS
+    lag = jnp.where(outer, lag3 + 1, lag2 + 1)
 
     def step(t, carry):
         @pl.when(t < nt)
         def _():
             expand(t)
 
-        @pl.when(inner & (t >= 1) & (t - 1 < nt))
-        def _():
-            join_first(t - 1)
-
-        @pl.when(inner & (t >= 2) & (t - 2 < nt))
-        def _():
-            join_second(t - 2)
-
-        @pl.when(outer & (t >= 4) & (t - 4 < nt))
-        def _():
-            join_third(t - 4)
-
-        j = t // nsub + 1
-
-        @pl.when((lax.rem(t, nsub) == nsub - 1) & (j >= nbc) & (j < nch))
-        def _():
-            turned_arrival(j).wait_recv()
-            produce(j)
+        @pl.when(inner & (t >= lag1) & (t - lag1 < nt))
+        def _():
+            join_first(t - lag1)
+
+        @pl.when(inner & (t >= lag2) & (t - lag2 < nt))
+        def _():
+            join_second(t - lag2)
+
+        @pl.when(outer & (t >= lag3) & (t - lag3 < nt))
+        def _():
+            join_third(t - lag3)
+
+        j = (t + ahead) // nsub
+
+        @pl.when((t >= 0) & (lax.rem(t + ahead, nsub) == 0) & (j < nch))
+        def _():
+            @pl.when(j < nbc)
+            def _():
+                for q in range(1, nbc):
+
+                    @pl.when(j == q)
+                    def _():
+                        load_turned(q).wait()
+
+            @pl.when(j >= nbc)
+            def _():
+                turned_arrival(j).wait_recv()
+
+            load_own(j).wait()
+            for h in range(nbc):
+                produce(j, h)
             reload(j + 2)
 
+        @pl.when(t + ahead < nt)
+        def _():
+            share(t + ahead)
+
+        for q in range(1, nbc):
+
+            @pl.when(t == q * nt // (2 * nbc) + SHIFT)
+            def _():
+                for o in range(1, X):
+                    turned_copy(o, q - 1).wait_send()
+                    turned_copy(o, q).start()
+
+        @pl.when(t == 2)
+        def _():
+            prepare()
+
         done = t - lag
 
-        @pl.when((done >= 0) & (lax.rem(done + nsub, nsub) == nsub - 1))
+        @pl.when((done >= 0) & (done < nt) & (lax.rem(done + nsub, nsub) == nsub - 1))
         def _():
             project(done // nsub)
 
         return carry
 
-    lax.fori_loop(0, nt + lag, step, 0)
+    lax.fori_loop(0, nt + lag3 + 1, step, 0)
 
     for k in range(kd):
         for m in range(2):
 
-            def bands(b, carry):
-                rows = pl.ds(pl.multiple_of(b * LANES, LANES), LANES)
-                sums[x, pl.ds(2 * k + m, 1), rows] = to_row(acc[k, m, rows, :])
-                return carry
-
-            lax.fori_loop(0, NB // LANES, bands, 0)
+            for b in range(NB // LANES):
+                rows = pl.ds(b * LANES, LANES)
+                sums[x, pl.ds(m * kd + k, 1), rows] = to_row(acc[k, m, rows, :])
 
     def sum_copy(o):
         to = lax.rem(x + o, X)
@@ -405,14 +463,10 @@
     total = sums[0]
     for o in range(1, X):
         total = total + sums[o]
-    for k in range(kd):
-        norm = total[2 * kd + k : 2 * kd + k + 1]
-        energy_ref[k : k + 1, :] = total[2 * k : 2 * k + 1] / norm
-        slope_ref[k : k + 1, :] = total[2 * k + 1 : 2 * k + 2] / norm
-
-    for q in range(nbc):
-        for o in range(1, X):
-            turned_copy(o, q).wait_send()
+    out_ref[...] = total
+
+    for o in range(1, X):
+        turned_copy(o, nbc - 1).wait_send()
     for o in range(1, X):
         sum_copy(o).wait_send()
 
@@ -421,7 +475,7 @@
             share_copy(t, o).wait_send()
             deal_copy(t, o).wait_send()
 
-        @pl.when(outer)
+        @pl.when(outer & (t >= nt - flight))
         def _():
             first_copy(t).wait_send()
 
@@ -442,7 +496,7 @@
         return False
     group = row // LINE
     nbc, span = nb // LANES, group * SUB
-    return group > 1 and nbc >= 2 and nb % span == 0 and (span <= LANES or span % LANES == 0) and bands % 256 == 0
+    return group > 1 and nbc >= 2 and LANES % span == 0 and bands % 256 == 0
 
 
 def one_kernel(hopping, lattice, kgrid, tangent, states):
@@ -452,21 +506,19 @@
     nbc = nb // LANES
     nch = X * nbc
     nt = nch * nb // (G * SUB)
-    coef = coefficients(lattice, kgrid, tangent, G, per)
-    kb = coef.shape[0] // LINE
-    cols = coef.shape[1]
+    kb = 2 * kgrid.shape[1] // LINE
+    cols = 2 * G * per
     slots = nbc
     tile = (SUB, LANES)
     dma = pltpu.SemaphoreType.DMA
-    out = jax.ShapeDtypeStruct((kd, NB), F32)
     vmem = pl.BlockSpec(memory_space=pltpu.VMEM)
     hbm = pl.BlockSpec(memory_space=pl.ANY)
     rows_of_sums = -(-3 * kd // 8) * 8
-    return pl.pallas_call(
+    total = pl.pallas_call(
         functools.partial(kernel, (X, G, per, nb, kd, NB)),
-        out_shape=(out, out),
-        in_specs=[vmem, hbm, hbm],
-        out_specs=(vmem, vmem),
+        out_shape=jax.ShapeDtypeStruct((rows_of_sums, NB), F32),
+        in_specs=[vmem, vmem, vmem, hbm, hbm],
+        out_specs=vmem,
         scratch_shapes=[
             pltpu.VMEM((LINE * kb, 3 * cols), BF16),
             pltpu.VMEM((2, 2, per, nb, LANES), F32),
@@ -503,7 +555,16 @@
         compiler_params=pltpu.CompilerParams(
             collective_id=0, has_side_effects=True, vmem_limit_bytes=67043328
         ),
-    )(coef, hopping, states)
+    )(lattice, kgrid, tangent, hopping, states)
+    norm = total[2 * kd : 3 * kd]
+    return total[: kd] / norm, total[kd : 2 * kd] / norm
+
+
+def phases(kgrid, lattice, tangent):
+    turns = jnp.mod(jnp.sum(kgrid[:, :, None] * lattice[:, None, :], axis=0), KGRID)
+    angle = turns.astype(jnp.float32) * (2.0 * math.pi / KGRID)
+    weight = jnp.sum(tangent[:, :, None] * lattice[:, None, :].astype(jnp.float32), axis=0)
+    return (jnp.cos(angle), jnp.sin(angle), weight)
 
 
 def project(m_re, m_im, rows, cols):

time: 184 us -> 174 us (0.946)
  Pallas kernels: 177 us -> 171 us
  local copies, waits for them, and re-layouts: 3.27 us -> 0 us
    pallas_call x1, Pallas kernels: 177 us -> 171 us  [one_kernel(): pl.pallas_call(functools.partial(kernel, (X, G, per, nb, kd, NB)), out_sh...]
    unnamed x2 -> x0, local copies, waits for them, and re-layouts: 2.59 us -> none
where the time goes in v2:
time: 174 us; the launch traced here: 173 us
  Pallas kernels  171 us (98%)
    pallas_call x1, Pallas kernels, one_kernel(): pl.pallas_call(functools.partial(kernel, (X, G, per, nb, kd, NB)), out_sh...  171 us

profile of v2, /device:TPU:0, one launch (start us, length us, event | category | flops | bytes accessed | tf_op | source)
XLA Modules:
  0.0 173.4 jit_solution(1639331364624829364)
XLA Ops:
  0.6 171.3 %shard_map.68 = f32[8,1024]{1,0:T(8,128)} custom-call(s32[3,128]{1,0:T(4,128)} %lattice_ref.1, s32[3,32]{1,0:T(4,128)} %kgrid_ref.1, f32[3,32]{1,0:T(4,128)} %tangent_ref.1, f32[2,8,256,512]{3,2,1,0:T(8,128)} %hop.1, f32[2,2,1024,512]{3,2,1,0:T(8,128)} %states.1), custom_call_target="tpu_custom_call" | custom-call | tf_op jit(solution)/shard_map/pallas_call | solution.py:517
  172.0 1.5 slice_divide_fusion

commit v3 on v2

--- a/solution.py
+++ b/solution.py
@@ -10,7 +10,8 @@
 
 KGRID = 8
 AHEAD = 2
-FLIGHT = 2
+FLIGHT = 3
+LATE = 4
 LAGS = (1, 3, 8)
 SHIFT = 1
 LINE = 4
@@ -107,6 +108,8 @@
     dr,
     es,
     er,
+    s0,
+    r0,
 ):
     X, G, per, nb, kd, NB = dims
     nbc = nb // LANES
@@ -175,7 +178,10 @@
         return remote(uvs.at[t, source], uva.at[t, source], gs.at[t, o - 1], gr.at[t, o - 1], at(a, source))
 
     def first_copy(t):
-        return remote(part.at[t, pl.ds(1, 3)], got1.at[t], s1.at[t], r1.at[t], at(beside, g))
+        return remote(part.at[t, pl.ds(2, 2)], got1.at[t, pl.ds(1, 2)], s1.at[t], r1.at[t], at(beside, g))
+
+    def late_copy(t):
+        return remote(part.at[t, 1], got1.at[t, 0], s0.at[t], r0.at[t], at(beside, g))
 
     def second_copy(t):
         return remote(part.at[t, pl.ds(2, 2)], got2.at[t], s2.at[t], r2.at[t], at(across, g))
@@ -285,7 +291,7 @@
 
     def join_first(t):
         first_copy(t).wait_recv()
-        part[t, 1:4] += got1[t]
+        part[t, 2:4] += got1[t, 1:3]
         second_copy(t).start()
 
     def join_second(t):
@@ -293,6 +299,17 @@
         part[t, 0] += got2[t, 1]
         third_copy(t).start()
         part[t, 1] += got2[t, 0]
+
+    def send_late(t):
+        @pl.when(t >= flight)
+        def _():
+            late_copy(t - flight).wait_send()
+
+        late_copy(t).start()
+
+    def join_late(t):
+        late_copy(t).wait_recv()
+        part[t, 1] += got1[t, 0]
         deal(t)
 
     def join_third(t):
@@ -375,7 +392,8 @@
     reload(2)
 
     lag1, lag2, lag3 = LAGS
-    lag = jnp.where(outer, lag3 + 1, lag2 + 1)
+    lag4 = LATE + 2
+    lag = jnp.where(outer, lag3, lag4) + 1
 
     def step(t, carry):
         @pl.when(t < nt)
@@ -389,6 +407,14 @@
         @pl.when(inner & (t >= lag2) & (t - lag2 < nt))
         def _():
             join_second(t - lag2)
+
+        @pl.when(inner & (t >= lag4) & (t - lag4 < nt))
+        def _():
+            join_late(t - lag4)
+
+        @pl.when(outer & (t >= LATE) & (t - LATE < nt))
+        def _():
+            send_late(t - LATE)
 
         @pl.when(outer & (t >= lag3) & (t - lag3 < nt))
         def _():
@@ -439,7 +465,7 @@
 
         return carry
 
-    lax.fori_loop(0, nt + lag3 + 1, step, 0)
+    lax.fori_loop(0, nt + max(lag3, lag4) + 1, step, 0)
 
     for k in range(kd):
         for m in range(2):
@@ -478,6 +504,7 @@
         @pl.when(outer & (t >= nt - flight))
         def _():
             first_copy(t).wait_send()
+            late_copy(t).wait_send()
 
         @pl.when(inner)
         def _():
@@ -551,6 +578,8 @@
             dma((nt, G - 1)),
             dma((X - 1,)),
             dma((X - 1,)),
+            dma((nt,)),
+            dma((nt,)),
         ],
         compiler_params=pltpu.CompilerParams(
             collective_id=0, has_side_effects=True, vmem_limit_bytes=67043328

time: 174 us -> 170 us (0.977)
  Pallas kernels: 171 us -> 167 us
    pallas_call x1, Pallas kernels: 171 us -> 167 us  [one_kernel(): pl.pallas_call(functools.partial(kernel, (X, G, per, nb, kd, NB)), out_sh...]
where the time goes in v3:
time: 170 us; the launch traced here: 169 us
  Pallas kernels  167 us (98%)
    pallas_call x1, Pallas kernels, one_kernel(): pl.pallas_call(functools.partial(kernel, (X, G, per, nb, kd, NB)), out_sh...  167 us

profile of v3, /device:TPU:0, one launch (start us, length us, event | category | flops | bytes accessed | tf_op | source)
XLA Modules:
  0.0 169.4 jit_solution(6449297058759359506)
XLA Ops:
  0.6 167.3 %shard_map.68 = f32[8,1024]{1,0:T(8,128)} custom-call(s32[3,128]{1,0:T(4,128)} %lattice_ref.1, s32[3,32]{1,0:T(4,128)} %kgrid_ref.1, f32[3,32]{1,0:T(4,128)} %tangent_ref.1, f32[2,8,256,512]{3,2,1,0:T(8,128)} %hop.1, f32[2,2,1024,512]{3,2,1,0:T(8,128)} %states.1), custom_call_target="tpu_custom_call" | custom-call | tf_op jit(solution)/shard_map/pallas_call | solution.py:544
  168.0 1.5 slice_divide_fusion
